TPU v7x, 64 devices: a 2x2x8 block of a 4x4x8 slice. The times are simulated.
64 devices in a mesh: dp: 4 (over x, y), kv: 16 (over z, core).
Axes of the slice: x: 2, y: 2, z: 8, core: 2. Of those that a mesh axis runs over, the one named last changes fastest.
The devices are a block of a 4x4x8 slice.
Arguments:
- x_first: bfloat16 [64, 4096], P('dp'), parts along dimension 0
- next_emb: bfloat16 [2, 64, 4096], P(None, 'dp'), parts along dimension 1
- k_cache: bfloat16 [64, 4096, 4, 128], P('dp', 'kv'), parts along dimension 0
- v_cache: bfloat16 [64, 4096, 4, 128], P('dp', 'kv'), parts along dimension 0
- seq_len: int32 [64], P('dp'), parts along dimension 0
- ln1_gain: float32 [4096], replicated
- ln1_bias: float32 [4096], replicated
- w_q: bfloat16 [4096, 2048], replicated
- b_q: float32 [2048], replicated
- w_k: bfloat16 [4096, 512], replicated
- b_k: float32 [512], replicated
- w_v: bfloat16 [4096, 512], replicated
- b_v: float32 [512], replicated
- w_o: bfloat16 [2048, 4096], replicated
- b_o: float32 [4096], replicated
- ln2_gain: float32 [4096], replicated
- ln2_bias: float32 [4096], replicated
- w_router: bfloat16 [4096, 16], replicated
- w_gate: bfloat16 [16, 4096, 448], P(None, None, 'kv')
- w_up: bfloat16 [16, 4096, 448], P(None, None, 'kv')
- w_down: bfloat16 [16, 448, 4096], P(None, 'kv')
- long_factor: float32 [64], replicated
- expert_idx: int32 [3, 64, 2], P(None, 'dp'), parts along dimension 1
- route_mask: int32 [3, 64, 2, 16], P(None, 'dp'), parts along dimension 1
Outputs:
- output 1: bfloat16 [3, 64, 4096], P(None, 'dp'), parts along dimension 1
- output 2: bfloat16 [64, 3, 4, 128], P('dp'), parts along dimension 0
- output 3: bfloat16 [64, 3, 4, 128], P('dp'), parts along dimension 0
There are 4 independent parts. A program takes and returns all parts, laid end to end along the dimension named above; an argument that names none is the same for every part.
All inputs are finite; a program needn't handle non-finite values.
Results may differ from a plain program's by a relative error of at most 0.0117778.
Values sent between devices are 32-bit elements.
A program may use at most 768 MiB of HBM per device.

v0:
```python
import functools
import math

import jax
import jax.numpy as jnp
import numpy as np
from jax import lax
from jax.experimental import pallas as pl
from jax.experimental.pallas import tpu as pltpu
from jax.sharding import PartitionSpec as P

ROPE_BASE = 10000.0
ROPE_MSCALE = math.sqrt(1.0 + math.log(32.0) / math.log(4096.0))
NORM_EPS = 1e-5
NEG_FILL = -1e30
MESH = pl.DeviceIdType.MESH
F32 = jnp.float32
BF16 = jnp.bfloat16
GROUPS = 2
K_CHUNKS = 8
TILE = 128


def iota(shape, dim):
    return lax.broadcasted_iota(jnp.int32, shape, dim)


def layer_norm_rows(x_f32, gain, bias):
    inv = 1.0 / x_f32.shape[-1]
    mean = jnp.sum(x_f32, axis=-1, keepdims=True) * inv
    centered = x_f32 - mean
    var = jnp.sum(centered * centered, axis=-1, keepdims=True) * inv
    return (centered * lax.rsqrt(var + NORM_EPS) * gain + bias).astype(BF16)


def dot_nt(a, b):
    return lax.dot_general(a, b, (((1,), (1,)), ((), ())), preferred_element_type=F32)


def dot_nn(a, b):
    return jnp.dot(a, b, preferred_element_type=F32)


def kernel(
    group,
    x_first, next_emb, kc, vc, seq_len, ln1_g, ln1_b, wq, bq, wk, bk, wv, bv, wo, bo, ln2_g, ln2_b, wr,
    wg, wu, wd, long_factor, powers, idx, mask,
    hidden, tail_k, tail_v,
    xbuf, hbuf, ln1g_v, ln1b_v, ln2g_v, ln2b_v, bo_v, bq_v, bk_v, bv_v, lf_v, pw_v, wr_v, idx_v, mask_v,
    wq_v, wk_v, wv_v, kc_v, vc_v, wo_v, acc_q, acc_k, acc_v, q2, k2, v2, tcol,
    stat, d2d1, rs1_send, rs1, obuf, osum, xmid, h2, act_g, act_u, pbuf, d2d2, sbuf, rs2, ybuf,
    small_sem, qkv_sem, kv_sem, wo_sem, moe_sem,
    d2d1_sem, rs1_sem, ag1_sem, fw1_sem, d2d2_sem, rs2_sem, ag2_sem, fw2_sem,
):
    batch, width = x_first.shape
    steps = next_emb.shape[0] + 1
    rows = steps * batch
    chips = group // 2
    q_heads = wq.shape[1] // TILE
    kv_heads = wk.shape[1] // TILE
    nb = batch // GROUPS
    spc = nb // chips
    rg = steps * nb
    half = q_heads * steps // 2
    qrows = 2 * half
    keys = kc.shape[1]
    shard_len = keys // kv_heads
    kstep = width // K_CHUNKS
    ff = wg.shape[0]
    experts = wr.shape[0]
    block = width // group
    scale = TILE ** -0.5

    me = lax.axis_index("kv")
    chip = lax.div(me, 2)
    core = lax.rem(me, 2)
    partner = me + 1 - 2 * core
    other = 1 - core

    def peer_chip(d):
        return lax.rem(chip + d, chips)

    def peer(d):
        return peer_chip(d) * 2 + core

    order = sorted(range(1, chips), key=lambda d: -min(d, chips - d))
    arrive = sorted(range(1, chips), key=lambda d: min(d, chips - d))

    barrier = pltpu.get_barrier_semaphore()
    pl.semaphore_signal(barrier, inc=1, device_id={"kv": partner}, device_id_type=MESH)
    for d in order:
        pl.semaphore_signal(barrier, inc=1, device_id={"kv": peer(d)}, device_id_type=MESH)

    smalls = [
        (x_first, xbuf.at[0]), (next_emb, xbuf.at[pl.ds(1, steps - 1)]), (ln1_g, ln1g_v), (ln1_b, ln1b_v),
        (long_factor, lf_v), (powers, pw_v), (bq, bq_v), (bk, bk_v), (bv, bv_v), (bo, bo_v),
        (ln2_g, ln2g_v), (ln2_b, ln2b_v), (wr, wr_v), (idx, idx_v), (mask, mask_v),
    ]
    small_copies = [pltpu.make_async_copy(src, dst, small_sem.at[i]) for i, (src, dst) in enumerate(smalls)]
    for copy in small_copies[:6]:
        copy.start()

    def qkv_copies(k):
        span = pl.ds(k * kstep, kstep)
        return [
            pltpu.make_async_copy(wq.at[span], wq_v.at[k], qkv_sem.at[0, k]),
            pltpu.make_async_copy(wk.at[span], wk_v.at[k], qkv_sem.at[1, k]),
            pltpu.make_async_copy(wv.at[span], wv_v.at[k], qkv_sem.at[2, k]),
        ]

    for k in range(K_CHUNKS):
        for copy in qkv_copies(k):
            copy.start()
    for copy in small_copies[6:]:
        copy.start()
    kv_copies = []
    for g in range(GROUPS):
        span = pl.ds(g * nb, nb)
        kv_copies.append([
            pltpu.make_async_copy(kc.at[span], kc_v.at[span], kv_sem.at[0, g]),
            pltpu.make_async_copy(vc.at[span], vc_v.at[span], kv_sem.at[1, g]),
        ])
        for copy in kv_copies[-1]:
            copy.start()
    wo_copy = pltpu.make_async_copy(wo, wo_v, wo_sem.at[0])
    wo_copy.start()

    row_k = iota((qrows, keys), 0)
    col_k = iota((qrows, keys), 1)
    head_of_row = (row_k * 43) >> 9
    pos = me * shard_len + (col_k >> 2)
    tcol[...] = jnp.where(head_of_row == (col_k & 3), pos, jnp.int32(1 << 30))

    for copy in small_copies[:6]:
        copy.wait()
    lane = iota((batch, TILE), 1)
    sub = iota((batch, TILE), 0)
    lens = jnp.zeros((batch, TILE), jnp.int32)
    for b in range(batch):
        lens = jnp.where(sub == b, seq_len[b], lens)
    lf = jnp.concatenate([lf_v[...], lf_v[...]], axis=1)
    inv_freq = 1.0 / (lf * pw_v[...])
    sign = jnp.where(lane < TILE // 2, -1.0, 1.0)
    cos_parts, sin_parts = [], []
    for s in range(steps):
        angles = (lens + s).astype(F32) * inv_freq
        cos_parts.append(jnp.cos(angles) * ROPE_MSCALE)
        sin_parts.append(jnp.sin(angles) * ROPE_MSCALE * sign)
    cos_full = jnp.concatenate(cos_parts, axis=0)
    sin_full = jnp.concatenate(sin_parts, axis=0)

    for s in range(steps):
        hbuf[s] = layer_norm_rows(xbuf[s].astype(F32), ln1g_v[...], ln1b_v[...])

    acc_q[...] = jnp.zeros_like(acc_q)
    acc_k[...] = jnp.zeros_like(acc_k)
    acc_v[...] = jnp.zeros_like(acc_v)

    @pl.loop(0, K_CHUNKS)
    def _(k):
        for copy in qkv_copies(k):
            copy.wait()
        h = hbuf[:, :, pl.ds(pl.multiple_of(k * kstep, kstep), kstep)].reshape(rows, kstep)
        acc_q[...] += dot_nn(h, wq_v[k])
        acc_k[...] += dot_nn(h, wk_v[k])
        acc_v[...] += dot_nn(h, wv_v[k])

    moe_copies = []
    hw = width // 2
    for i, src in enumerate((wg, wu, wd)):
        for j in range(2):
            copy = pltpu.make_async_copy(src.at[:, pl.ds(j * hw, hw)], wq_v.at[2 * i + j, pl.ds(0, ff)], moe_sem.at[i, j])
            copy.start()
            moe_copies.append(copy)
    for copy in small_copies[6:]:
        copy.wait()

    def rotate(x):
        x = x.astype(BF16).astype(F32)
        return (x * cos_full + pltpu.roll(x, TILE // 2, 1) * sin_full).astype(BF16).astype(F32)

    for i in range(q_heads):
        cols = pl.ds(i * TILE, TILE)
        q2[pl.ds(i * rows, rows)] = rotate(acc_q[:, cols] + bq_v[:, cols])
    for i in range(kv_heads):
        cols = pl.ds(i * TILE, TILE)
        k_rot = rotate(acc_k[:, cols] + bk_v[:, cols])
        v_new = (acc_v[:, cols] + bv_v[:, cols]).astype(BF16)
        k2[pl.ds(i * rows, rows)] = k_rot
        v2[pl.ds(i * rows, rows)] = v_new.astype(F32)
        for s in range(steps):
            tail_k[i, s] = k_rot[s * batch:(s + 1) * batch].astype(BF16)
            tail_v[i, s] = v_new[s * batch:(s + 1) * batch]
    k2[pl.ds(kv_heads * rows, k2.shape[0] - kv_heads * rows)] = jnp.zeros((k2.shape[0] - kv_heads * rows, TILE), F32)
    v2[pl.ds(kv_heads * rows, v2.shape[0] - kv_heads * rows)] = jnp.zeros((v2.shape[0] - kv_heads * rows, TILE), F32)

    eye = iota((half, TILE), 0) == iota((half, TILE), 1)
    sub8 = iota((8, TILE), 0)

    def to_row(col):
        return jnp.sum(jnp.where(eye, jnp.broadcast_to(col, (half, TILE)), 0.0), axis=0, keepdims=True)

    def to_col(row):
        return jnp.sum(jnp.where(eye, jnp.broadcast_to(row, (half, TILE)), 0.0), axis=1, keepdims=True)

    def pair_tile(m_row, l_row):
        return jnp.where(sub8 == 0, m_row, jnp.where(sub8 == 1, l_row, 0.0))

    def attend(b):
        q = q2[pl.ds(b, qrows, stride=batch)].astype(BF16)
        scores = dot_nt(q, kc_v[b]) * scale
        keep = tcol[...] < seq_len[b]
        scores = jnp.where(keep, scores, NEG_FILL)
        top = jnp.max(scores, axis=1, keepdims=True)
        w = jnp.where(keep, jnp.exp(scores - top), 0.0)
        total = jnp.sum(w, axis=1, keepdims=True)
        out = dot_nn(w.astype(BF16), vc_v[b])
        for hf in range(2):
            part = slice(hf * half, (hf + 1) * half)
            stat[hf, b, pl.ds(0, half)] = out[part]
            stat[hf, b, pl.ds(half, 8)] = pair_tile(to_row(top[part]), to_row(total[part]))

    sends = []

    def send(src, dst, sems, slot, device):
        copy = pltpu.make_async_remote_copy(
            src_ref=src, dst_ref=dst, send_sem=sems.at[(0,) + slot], recv_sem=sems.at[(1,) + slot],
            device_id={"kv": device}, device_id_type=MESH)
        copy.start()
        sends.append(copy)
        return copy

    d2d1_copies, rs1_copies, ag1_copies, fw1_copies = {}, {}, {}, {}
    d2d2_copies, rs2_copies, ag2_copies, fw2_copies = {}, {}, {}, {}

    def merge_pair(b):
        own, got = stat[core, b], d2d1[b]
        m1, l1 = own[half:half + 1], own[half + 1:half + 2]
        m2, l2 = got[half:half + 1], got[half + 1:half + 2]
        top = jnp.maximum(m1, m2)
        a1, a2 = jnp.exp(m1 - top), jnp.exp(m2 - top)
        rs1_send[b, pl.ds(0, half)] = own[:half] * to_col(a1) + got[:half] * to_col(a2)
        rs1_send[b, pl.ds(half, 8)] = pair_tile(top, l1 * a1 + l2 * a2)

    def start_d2d1(g):
        span = pl.ds(g * nb, nb)
        d2d1_copies[g] = send(stat.at[other, span], d2d1.at[span], d2d1_sem, (g,), partner)

    def start_rs1(g):
        d2d1_copies[g].wait_recv()
        for i in range(nb):
            merge_pair(g * nb + i)
        for d in order:
            span = pl.ds(g * nb + peer_chip(d) * spc, spc)
            rs1_copies[g, d] = send(rs1_send.at[span], rs1.at[g, d], rs1_sem, (g, d), peer(d))

    def tail_stats(b):
        q = q2[pl.ds(b + core * (half * batch), half, stride=batch)].astype(BF16)
        k = k2[pl.ds(b, 16, stride=batch)].astype(BF16)
        v = v2[pl.ds(b, 16, stride=batch)].astype(BF16)
        r, j = iota((half, 16), 0), iota((half, 16), 1)
        r3, j3 = (r * 43) >> 7, (j * 43) >> 7
        head = core * (kv_heads // 2) + (r3 >> 2)
        keep = (j3 == head) & ((j - j3 * steps) <= (r - r3 * steps))
        scores = jnp.where(keep, dot_nt(q, k) * scale, NEG_FILL)
        top = jnp.max(scores, axis=1, keepdims=True)
        w = jnp.where(keep, jnp.exp(scores - top), 0.0)
        total = jnp.sum(w, axis=1, keepdims=True)
        return dot_nn(w.astype(BF16), v), to_row(top), to_row(total)

    def start_ag1(g):
        tails = [tail_stats(g * nb + chip * spc + i) for i in range(spc)]
        for d in arrive:
            rs1_copies[g, d].wait_recv()
        for i in range(spc):
            b = g * nb + chip * spc + i
            own = rs1_send[b]
            units = [tails[i], (own[:half], own[half:half + 1], own[half + 1:half + 2])]
            for d in arrive:
                got = rs1[g, d, i]
                units.append((got[:half], got[half:half + 1], got[half + 1:half + 2]))
            top = functools.reduce(jnp.maximum, [u[1] for u in units])
            o_sum, l_sum = 0.0, 0.0
            for o, m, l in units:
                a = jnp.exp(m - top)
                l_sum = l_sum + l * a
                o_sum = o_sum + o * to_col(a)
            obuf[g, core, chip, i] = o_sum / to_col(l_sum)
        own_ref = obuf.at[g, core, chip]
        for d in order:
            ag1_copies[g, d] = send(own_ref, own_ref, ag1_sem, (g, d), peer(d))
        fw1_copies[g, 0] = send(own_ref, own_ref, fw1_sem, (g, 0), partner)

    def forward1(g):
        for d in arrive:
            ag1_copies[g, d].wait_recv()
            ref = obuf.at[g, core, peer_chip(chips - d)]
            fw1_copies[g, d] = send(ref, ref, fw1_sem, (g, d), partner)

    def finish1(g):
        for d in range(chips):
            fw1_copies[g, d].wait_recv()
        for hf in range(2):
            for i in range(q_heads // 2):
                parts = []
                for s in range(steps):
                    parts.append(osum_rows(g, hf, i * steps + s))
                col = hf * (q_heads // 2) + i
                osum[:, pl.ds(col * TILE, TILE)] = jnp.concatenate(parts, axis=0)

    def osum_rows(g, hf, r):
        return obuf_rows.at[g, hf][pl.ds(r, nb, stride=half)]

    obuf_rows = obuf.reshape(GROUPS, 2, nb * half, TILE)

    def project(g):
        o = osum[...].astype(BF16)
        x = xbuf[:, pl.ds(g * nb, nb)].astype(F32).reshape(rg, width)
        xmid[g] = x

        @pl.loop(0, K_CHUNKS)
        def _(n):
            cols = pl.ds(pl.multiple_of(n * kstep, kstep), kstep)
            val = xmid[g, :, cols] + dot_nn(o, wo_v[:, cols]) + bo_v[:, cols]
            xmid[g, :, cols] = val.astype(BF16).astype(F32)

        h2[...] = layer_norm_rows(xmid[g], ln2g_v[...], ln2b_v[...])

    def gates(g):
        logits = dot_nt(h2[...], wr_v[...])
        out = []
        e = iota((nb, experts), 1)
        pick = iota((nb, batch), 1) == iota((nb, batch), 0) + g * nb
        for s in range(steps):
            r = logits[s * nb:(s + 1) * nb]
            total = jnp.zeros((nb, experts), F32)
            for k in range(idx_v.shape[1]):
                allowed = mask_v[s, pl.ds(g * nb, nb), k, :] == 1
                masked = jnp.where(allowed, r, NEG_FILL)
                p = jnp.exp(masked - jnp.max(masked, axis=1, keepdims=True))
                p = p / jnp.sum(p, axis=1, keepdims=True)
                row = jnp.broadcast_to(idx_v[s, pl.ds(k, 1), :].astype(F32), (nb, batch))
                col = jnp.sum(jnp.where(pick, row, 0.0), axis=1, keepdims=True)
                total = total + jnp.where(col == e.astype(F32), p, 0.0)
            out.append(total)
        gate = jnp.concatenate(out, axis=0)
        gate = jnp.concatenate([gate, jnp.zeros((rg, TILE - experts), F32)], axis=1)
        shift = experts
        while shift < TILE:
            gate = gate + pltpu.roll(gate, shift, 1)
            shift *= 2
        reps = -(-ff // TILE)
        return jnp.concatenate([gate] * reps, axis=1)[:, :ff]

    def expert_parts(g):
        gate = gates(g)
        act_g[...] = jnp.zeros_like(act_g)
        act_u[...] = jnp.zeros_like(act_u)
        per = K_CHUNKS // 2

        @pl.loop(0, 2)
        def _(j):
            @pl.loop(0, per)
            def _(k):
                src = pl.ds(pl.multiple_of(j * hw + k * kstep, kstep), kstep)
                cols = pl.ds(pl.multiple_of(k * kstep, kstep), kstep)
                h = h2[:, src]
                act_g[...] += dot_nt(h, wq_v[j, pl.ds(0, ff), cols])
                act_u[...] += dot_nt(h, wq_v[2 + j, pl.ds(0, ff), cols])

        ag = act_g[...]
        u = (gate * (ag * (1.0 / (1.0 + jnp.exp(-ag)))) * act_u[...]).astype(BF16)

        @pl.loop(0, 2)
        def _(j):
            @pl.loop(0, per)
            def _(k):
                cols = pl.ds(pl.multiple_of(k * kstep, kstep), kstep)
                part = dot_nn(u, wq_v[4 + j, pl.ds(0, ff), cols]).astype(BF16).astype(F32)
                pair = j * per + k
                pbuf[g, 0, pair] = part[:, :block]
                pbuf[g, 1, pair] = part[:, block:]

        d2d2_copies[g] = send(pbuf.at[g, other], d2d2.at[g], d2d2_sem, (g,), partner)

    def start_rs2(g):
        d2d2_copies[g].wait_recv()
        for d in order:
            z = peer_chip(d)
            sbuf[g, z] = pbuf[g, core, z] + d2d2[g, z]
            rs2_copies[g, d] = send(sbuf.at[g, z], rs2.at[g, d], rs2_sem, (g, d), peer(d))

    def start_ag2(g):
        total = pbuf[g, core, chip] + d2d2[g, chip]
        for d in arrive:
            rs2_copies[g, d].wait_recv()
            total = total + rs2[g, d]
        x = xmid[g, :, pl.ds(pl.multiple_of(me * block, block), block)]
        ybuf[g, core, chip] = (x + total).astype(BF16).astype(F32)
        own_ref = ybuf.at[g, core, chip]
        for d in order:
            ag2_copies[g, d] = send(own_ref, own_ref, ag2_sem, (g, d), peer(d))
        fw2_copies[g, 0] = send(own_ref, own_ref, fw2_sem, (g, 0), partner)

    def forward2(g):
        for d in arrive:
            ag2_copies[g, d].wait_recv()
            ref = ybuf.at[g, core, peer_chip(chips - d)]
            fw2_copies[g, d] = send(ref, ref, fw2_sem, (g, d), partner)

    for g in range(GROUPS):
        for copy in kv_copies[g]:
            copy.wait()

        @pl.loop(0, nb // 4)
        def _(i):
            for j in range(4):
                attend(g * nb + i * 4 + j)

        if g == 0:
            pl.semaphore_wait(barrier, chips)
        start_d2d1(g)
        if g > 0:
            start_rs1(g - 1)
    start_rs1(GROUPS - 1)
    for g in range(GROUPS):
        start_ag1(g)
    wo_copy.wait()
    for copy in moe_copies:
        copy.wait()
    for g in range(GROUPS):
        forward1(g)
        finish1(g)
        project(g)
        expert_parts(g)
        start_rs2(g)
    for g in range(GROUPS):
        start_ag2(g)
    for g in range(GROUPS):
        forward2(g)
    for g in range(GROUPS):
        for d in range(chips):
            fw2_copies[g, d].wait_recv()
    for z in range(chips):
        for c in range(2):
            cols = pl.ds((z * 2 + c) * block, block)
            for s in range(steps):
                parts = [ybuf[g, c, z, pl.ds(s * nb, nb)] for g in range(GROUPS)]
                hidden[s, :, cols] = jnp.concatenate(parts, axis=0).astype(BF16)
    for copy in sends:
        copy.wait_send()


def solution(mesh):
    group = mesh.shape["kv"]
    chips = group // 2

    def layer_steps(x_first, next_emb, k_cache, v_cache, seq_len, ln1_gain, ln1_bias, w_q, b_q, w_k, b_k, w_v, b_v, w_o, b_o, ln2_gain, ln2_bias, w_router, w_gate, w_up, w_down, long_factor, expert_idx, route_mask):
        batch, shard_len, kv_heads, head_dim = k_cache.shape
        width = x_first.shape[1]
        steps = next_emb.shape[0] + 1
        q_heads = w_q.shape[1] // head_dim
        experts, _, ff_local = w_gate.shape
        ff = experts * ff_local
        rows = steps * batch
        half = q_heads * steps // 2
        keys = shard_len * kv_heads
        nb = batch // GROUPS
        spc = nb // chips
        rg = steps * nb
        block = width // group
        kstep = width // K_CHUNKS
        exponent = np.arange(head_dim // 2, dtype=np.float64) * 2.0 / head_dim
        powers = np.tile((ROPE_BASE ** exponent).astype(np.float32), 2)[None]

        row = lambda vec: vec.reshape(1, -1)
        flat = lambda arr: arr.reshape(batch, keys, head_dim)
        operands = (
            x_first, next_emb, flat(k_cache), flat(v_cache), seq_len, row(ln1_gain), row(ln1_bias),
            w_q, row(b_q), w_k, row(b_k), w_v, row(b_v), w_o, row(b_o), row(ln2_gain), row(ln2_bias), w_router.T,
            w_gate.transpose(2, 0, 1).reshape(ff, width), w_up.transpose(2, 0, 1).reshape(ff, width),
            w_down.transpose(1, 0, 2).reshape(ff, width), row(long_factor), jnp.asarray(powers),
            expert_idx.transpose(0, 2, 1), route_mask,
        )
        any_spec = pl.BlockSpec(memory_space=pl.ANY)
        in_specs = [any_spec] * len(operands)
        in_specs[4] = pl.BlockSpec(memory_space=pltpu.SMEM)
        vmem = pl.BlockSpec(memory_space=pltpu.VMEM)
        V = pltpu.VMEM
        dma = pltpu.SemaphoreType.DMA
        scratch = [
            V((steps, batch, width), BF16), V((steps, batch, width), BF16),
            V((1, width), F32), V((1, width), F32), V((1, width), F32), V((1, width), F32), V((1, width), F32),
            V((1, q_heads * head_dim), F32), V((1, kv_heads * head_dim), F32), V((1, kv_heads * head_dim), F32),
            V((1, head_dim // 2), F32), V((1, head_dim), F32), V((experts, width), BF16),
            V((steps, expert_idx.shape[2], batch), jnp.int32), V(route_mask.shape, jnp.int32),
            V((K_CHUNKS, kstep, q_heads * head_dim), BF16),
            V((K_CHUNKS, kstep, kv_heads * head_dim), BF16), V((K_CHUNKS, kstep, kv_heads * head_dim), BF16),
            V((batch, keys, head_dim), BF16), V((batch, keys, head_dim), BF16), V(w_o.shape, BF16),
            V((rows, q_heads * head_dim), F32), V((rows, kv_heads * head_dim), F32), V((rows, kv_heads * head_dim), F32),
            V((q_heads * rows, head_dim), F32), V((16 * batch, head_dim), F32), V((16 * batch, head_dim), F32),
            V((2 * half, keys), jnp.int32),
            V((2, batch, half + 8, head_dim), F32), V((batch, half + 8, head_dim), F32), V((batch, half + 8, head_dim), F32),
            V((GROUPS, chips, spc, half + 8, head_dim), F32), V((GROUPS, 2, chips, spc, half, head_dim), F32),
            V((rg, q_heads * head_dim), F32), V((GROUPS, rg, width), F32), V((rg, width), BF16),
            V((rg, ff), F32), V((rg, ff), F32),
            V((GROUPS, 2, chips, rg, block), F32), V((GROUPS, chips, rg, block), F32), V((GROUPS, chips, rg, block), F32),
            V((GROUPS, chips, rg, block), F32), V((GROUPS, 2, chips, rg, block), F32),
            dma((15,)), dma((3, K_CHUNKS)), dma((2, GROUPS)), dma((1,)), dma((3, 2)),
            dma((2, GROUPS)), dma((2, GROUPS, chips)), dma((2, GROUPS, chips)), dma((2, GROUPS, chips)),
            dma((2, GROUPS)), dma((2, GROUPS, chips)), dma((2, GROUPS, chips)), dma((2, GROUPS, chips)),
        ]
        tail_shape = jax.ShapeDtypeStruct((kv_heads, steps, batch, head_dim), BF16)
        hidden, tail_k, tail_v = pl.pallas_call(
            functools.partial(kernel, group),
            out_shape=(jax.ShapeDtypeStruct((steps, batch, width), BF16), tail_shape, tail_shape),
            in_specs=in_specs,
            out_specs=(vmem, vmem, vmem),
            scratch_shapes=scratch,
            name="decode_layer",
            compiler_params=pltpu.CompilerParams(
                collective_id=0, has_side_effects=True, vmem_limit_bytes=66_000_000),
        )(*operands)
        order = (2, 1, 0, 3)
        return hidden, tail_k.transpose(order), tail_v.transpose(order)

    replicated = P()
    in_specs = (P('dp'), P(None, 'dp'), P('dp', 'kv'), P('dp', 'kv'), P('dp')) + (replicated,) * 13 + (P(None, None, 'kv'), P(None, None, 'kv'), P(None, 'kv'), replicated, P(None, 'dp'), P(None, 'dp'))
    out_specs = (P(None, 'dp'), P('dp'), P('dp'))
    return jax.shard_map(layer_steps, mesh=mesh, in_specs=in_specs, out_specs=out_specs, check_vma=False)
```

profile of v0, /device:TPU:21, one launch (start us, length us, event | category | flops | bytes accessed | tf_op | source)
XLA Modules:
  0.0 82.9 jit_solution(9391754863196564703)
XLA Ops:
  0.6 77.6 %decode_layer.1 = (bf16[3,16,4096]{2,1,0:T(8,128)(2,1)}, bf16[4,3,16,128]{3,2,1,0:T(8,128)(2,1)}, bf16[4,3,16,128]{3,2,1,0:T(8,128)(2,1)}) custom-call(bf16[16,4096]{1,0:T(8,128)(2,1)} %x_first.1, bf16[2,16,4096]{2,1,0:T(8,128)(2,1)} %next_emb.1, bf16[16,1024,128]{2,1,0:T(8,128)(2,1)} %bitcast.24, bf16[16,1024,128]{2,1,0:T(8,128)(2,1)} %bitcast.25, ...), custom_call_target="tpu_custom_call" | custom-call | tf_op jit(solution)/shard_map/decode_layer/pallas_call | solution.py:514
  78.2 1.4 %copy.28 = bf16[16,3,4,128]{3,2,1,0:T(4,128)(2,1)} copy(bf16[16,3,4,128]{3,0,1,2:T(8,128)(2,1)} %bitcast.31) | data formatting | bytes 98304
  79.7 1.4 %copy.29 = bf16[16,3,4,128]{3,2,1,0:T(4,128)(2,1)} copy(bf16[16,3,4,128]{3,0,1,2:T(8,128)(2,1)} %bitcast.30) | data formatting | bytes 98304
  81.1 1.8 %copy.31 = bf16[3,16,4096]{2,1,0:T(8,128)(2,1)} copy(bf16[3,16,4096]{2,1,0:T(8,128)(2,1)} %get-tuple-element.15) | data formatting | bytes 786432
where the time goes:
time: 83.1 us; the launch traced here: 82.9 us
  Pallas kernels  77.6 us (93%)
  local copies, waits for them, and re-layouts  4.64 us (6%)
    pallas_call x1, Pallas kernels, layer_steps(): pl.pallas_call(functools.partial(kernel, group), out_shape=(jax.ShapeDtyp...  77.6 us
    unnamed x3, local copies, waits for them, and re-layouts  4.64 us

commit v1 on v0

--- a/solution.py
+++ b/solution.py
@@ -1,3 +1,4 @@
+import contextlib
 import functools
 import math
 
@@ -17,6 +18,8 @@
 F32 = jnp.float32
 BF16 = jnp.bfloat16
 GROUPS = 2
+CHUNKS = 4
+scope = contextlib.nullcontext
 K_CHUNKS = 8
 TILE = 128
 
@@ -48,7 +51,7 @@
     hidden, tail_k, tail_v,
     xbuf, hbuf, ln1g_v, ln1b_v, ln2g_v, ln2b_v, bo_v, bq_v, bk_v, bv_v, lf_v, pw_v, wr_v, idx_v, mask_v,
     wq_v, wk_v, wv_v, kc_v, vc_v, wo_v, acc_q, acc_k, acc_v, q2, k2, v2, tcol,
-    stat, d2d1, rs1_send, rs1, obuf, osum, xmid, h2, act_g, act_u, pbuf, d2d2, sbuf, rs2, ybuf,
+    stat, d2d1, rs1_send, rs1, obuf, osum, xmid, h2, pbuf, d2d2, sbuf, rs2, ybuf,
     small_sem, qkv_sem, kv_sem, wo_sem, moe_sem,
     d2d1_sem, rs1_sem, ag1_sem, fw1_sem, d2d2_sem, rs2_sem, ag2_sem, fw2_sem,
 ):
@@ -60,7 +63,6 @@
     kv_heads = wk.shape[1] // TILE
     nb = batch // GROUPS
     spc = nb // chips
-    rg = steps * nb
     half = q_heads * steps // 2
     qrows = 2 * half
     keys = kc.shape[1]
@@ -68,7 +70,7 @@
     kstep = width // K_CHUNKS
     ff = wg.shape[0]
     experts = wr.shape[0]
-    block = width // group
+    block = width // group // 2
     scale = TILE ** -0.5
 
     me = lax.axis_index("kv")
@@ -108,11 +110,11 @@
             pltpu.make_async_copy(wv.at[span], wv_v.at[k], qkv_sem.at[2, k]),
         ]
 
+    for copy in small_copies[6:]:
+        copy.start()
     for k in range(K_CHUNKS):
         for copy in qkv_copies(k):
-            copy.start()
-    for copy in small_copies[6:]:
-        copy.start()
+            copy.start(priority=1)
     kv_copies = []
     for g in range(GROUPS):
         span = pl.ds(g * nb, nb)
@@ -121,9 +123,9 @@
             pltpu.make_async_copy(vc.at[span], vc_v.at[span], kv_sem.at[1, g]),
         ])
         for copy in kv_copies[-1]:
-            copy.start()
+            copy.start(priority=1)
     wo_copy = pltpu.make_async_copy(wo, wo_v, wo_sem.at[0])
-    wo_copy.start()
+    wo_copy.start(priority=1)
 
     row_k = iota((qrows, keys), 0)
     col_k = iota((qrows, keys), 1)
@@ -170,7 +172,7 @@
     for i, src in enumerate((wg, wu, wd)):
         for j in range(2):
             copy = pltpu.make_async_copy(src.at[:, pl.ds(j * hw, hw)], wq_v.at[2 * i + j, pl.ds(0, ff)], moe_sem.at[i, j])
-            copy.start()
+            copy.start(priority=1)
             moe_copies.append(copy)
     for copy in small_copies[6:]:
         copy.wait()
@@ -188,9 +190,8 @@
         v_new = (acc_v[:, cols] + bv_v[:, cols]).astype(BF16)
         k2[pl.ds(i * rows, rows)] = k_rot
         v2[pl.ds(i * rows, rows)] = v_new.astype(F32)
-        for s in range(steps):
-            tail_k[i, s] = k_rot[s * batch:(s + 1) * batch].astype(BF16)
-            tail_v[i, s] = v_new[s * batch:(s + 1) * batch]
+        tail_k[i] = k_rot
+        tail_v[i] = v_new.astype(F32)
     k2[pl.ds(kv_heads * rows, k2.shape[0] - kv_heads * rows)] = jnp.zeros((k2.shape[0] - kv_heads * rows, TILE), F32)
     v2[pl.ds(kv_heads * rows, v2.shape[0] - kv_heads * rows)] = jnp.zeros((v2.shape[0] - kv_heads * rows, TILE), F32)
 
@@ -231,7 +232,7 @@
         return copy
 
     d2d1_copies, rs1_copies, ag1_copies, fw1_copies = {}, {}, {}, {}
-    d2d2_copies, rs2_copies, ag2_copies, fw2_copies = {}, {}, {}, {}
+    d2d2_copies = {}
 
     def merge_pair(b):
         own, got = stat[core, b], d2d1[b]
@@ -297,54 +298,41 @@
             ref = obuf.at[g, core, peer_chip(chips - d)]
             fw1_copies[g, d] = send(ref, ref, fw1_sem, (g, d), partner)
 
-    def finish1(g):
-        for d in range(chips):
-            fw1_copies[g, d].wait_recv()
+    obuf_rows = obuf.reshape(GROUPS, 2, nb * half, TILE)
+
+    def project():
         for hf in range(2):
             for i in range(q_heads // 2):
-                parts = []
-                for s in range(steps):
-                    parts.append(osum_rows(g, hf, i * steps + s))
+                parts = [obuf_rows.at[g, hf][pl.ds(i * steps + s, nb, stride=half)]
+                         for s in range(steps) for g in range(GROUPS)]
                 col = hf * (q_heads // 2) + i
                 osum[:, pl.ds(col * TILE, TILE)] = jnp.concatenate(parts, axis=0)
-
-    def osum_rows(g, hf, r):
-        return obuf_rows.at[g, hf][pl.ds(r, nb, stride=half)]
-
-    obuf_rows = obuf.reshape(GROUPS, 2, nb * half, TILE)
-
-    def project(g):
         o = osum[...].astype(BF16)
-        x = xbuf[:, pl.ds(g * nb, nb)].astype(F32).reshape(rg, width)
-        xmid[g] = x
-
-        @pl.loop(0, K_CHUNKS)
-        def _(n):
-            cols = pl.ds(pl.multiple_of(n * kstep, kstep), kstep)
-            val = xmid[g, :, cols] + dot_nn(o, wo_v[:, cols]) + bo_v[:, cols]
-            xmid[g, :, cols] = val.astype(BF16).astype(F32)
-
-        h2[...] = layer_norm_rows(xmid[g], ln2g_v[...], ln2b_v[...])
-
-    def gates(g):
+        for n in range(2):
+            cols = pl.ds(n * hw, hw)
+            x = xbuf[:, :, cols].astype(F32).reshape(rows, hw)
+            val = x + dot_nn(o, wo_v[:, cols]) + bo_v[:, cols]
+            xmid[:, cols] = val.astype(BF16).astype(F32)
+        h2[...] = layer_norm_rows(xmid[...], ln2g_v[...], ln2b_v[...])
+
+    def gates():
         logits = dot_nt(h2[...], wr_v[...])
         out = []
-        e = iota((nb, experts), 1)
-        pick = iota((nb, batch), 1) == iota((nb, batch), 0) + g * nb
+        e = iota((batch, experts), 1).astype(F32)
+        pick = iota((batch, batch), 1) == iota((batch, batch), 0)
         for s in range(steps):
-            r = logits[s * nb:(s + 1) * nb]
-            total = jnp.zeros((nb, experts), F32)
+            r = logits[s * batch:(s + 1) * batch]
+            total = jnp.zeros((batch, experts), F32)
             for k in range(idx_v.shape[1]):
-                allowed = mask_v[s, pl.ds(g * nb, nb), k, :] == 1
-                masked = jnp.where(allowed, r, NEG_FILL)
+                masked = jnp.where(mask_v[s, :, k, :] == 1, r, NEG_FILL)
                 p = jnp.exp(masked - jnp.max(masked, axis=1, keepdims=True))
                 p = p / jnp.sum(p, axis=1, keepdims=True)
-                row = jnp.broadcast_to(idx_v[s, pl.ds(k, 1), :].astype(F32), (nb, batch))
+                row = jnp.broadcast_to(idx_v[s, pl.ds(k, 1), :].astype(F32), (batch, batch))
                 col = jnp.sum(jnp.where(pick, row, 0.0), axis=1, keepdims=True)
-                total = total + jnp.where(col == e.astype(F32), p, 0.0)
+                total = total + jnp.where(col == e, p, 0.0)
             out.append(total)
         gate = jnp.concatenate(out, axis=0)
-        gate = jnp.concatenate([gate, jnp.zeros((rg, TILE - experts), F32)], axis=1)
+        gate = jnp.concatenate([gate, jnp.zeros((rows, TILE - experts), F32)], axis=1)
         shift = experts
         while shift < TILE:
             gate = gate + pltpu.roll(gate, shift, 1)
@@ -352,103 +340,164 @@
         reps = -(-ff // TILE)
         return jnp.concatenate([gate] * reps, axis=1)[:, :ff]
 
-    def expert_parts(g):
-        gate = gates(g)
-        act_g[...] = jnp.zeros_like(act_g)
-        act_u[...] = jnp.zeros_like(act_u)
-        per = K_CHUNKS // 2
-
-        @pl.loop(0, 2)
-        def _(j):
-            @pl.loop(0, per)
-            def _(k):
-                src = pl.ds(pl.multiple_of(j * hw + k * kstep, kstep), kstep)
-                cols = pl.ds(pl.multiple_of(k * kstep, kstep), kstep)
-                h = h2[:, src]
-                act_g[...] += dot_nt(h, wq_v[j, pl.ds(0, ff), cols])
-                act_u[...] += dot_nt(h, wq_v[2 + j, pl.ds(0, ff), cols])
-
-        ag = act_g[...]
-        u = (gate * (ag * (1.0 / (1.0 + jnp.exp(-ag)))) * act_u[...]).astype(BF16)
-
-        @pl.loop(0, 2)
-        def _(j):
-            @pl.loop(0, per)
-            def _(k):
-                cols = pl.ds(pl.multiple_of(k * kstep, kstep), kstep)
-                part = dot_nn(u, wq_v[4 + j, pl.ds(0, ff), cols]).astype(BF16).astype(F32)
-                pair = j * per + k
-                pbuf[g, 0, pair] = part[:, :block]
-                pbuf[g, 1, pair] = part[:, block:]
-
-        d2d2_copies[g] = send(pbuf.at[g, other], d2d2.at[g], d2d2_sem, (g,), partner)
-
-    def start_rs2(g):
-        d2d2_copies[g].wait_recv()
-        for d in order:
-            z = peer_chip(d)
-            sbuf[g, z] = pbuf[g, core, z] + d2d2[g, z]
-            rs2_copies[g, d] = send(sbuf.at[g, z], rs2.at[g, d], rs2_sem, (g, d), peer(d))
-
-    def start_ag2(g):
-        total = pbuf[g, core, chip] + d2d2[g, chip]
-        for d in arrive:
-            rs2_copies[g, d].wait_recv()
-            total = total + rs2[g, d]
-        x = xmid[g, :, pl.ds(pl.multiple_of(me * block, block), block)]
-        ybuf[g, core, chip] = (x + total).astype(BF16).astype(F32)
-        own_ref = ybuf.at[g, core, chip]
-        for d in order:
-            ag2_copies[g, d] = send(own_ref, own_ref, ag2_sem, (g, d), peer(d))
-        fw2_copies[g, 0] = send(own_ref, own_ref, fw2_sem, (g, 0), partner)
-
-    def forward2(g):
-        for d in arrive:
-            ag2_copies[g, d].wait_recv()
-            ref = ybuf.at[g, core, peer_chip(chips - d)]
-            fw2_copies[g, d] = send(ref, ref, fw2_sem, (g, d), partner)
+    rhalf = rows // 2
+
+    def expert_parts():
+        gate = gates()
+        span = pl.ds(0, ff)
+        ag = dot_nt(h2[:, :hw], wq_v[0, span]) + dot_nt(h2[:, hw:], wq_v[1, span])
+        au = dot_nt(h2[:, :hw], wq_v[2, span]) + dot_nt(h2[:, hw:], wq_v[3, span])
+        u = (gate * (ag * (1.0 / (1.0 + jnp.exp(-ag)))) * au).astype(BF16)
+        for h in range(2):
+            part = dot_nn(u, wq_v[4 + h, span]).astype(BF16).astype(F32)
+            for j in range(group):
+                for r in range(2):
+                    pbuf[2 * h + r, j % 2, j // 2] = part[r * rhalf:(r + 1) * rhalf, j * block:(j + 1) * block]
+            for r in range(2):
+                q = 2 * h + r
+                d2d2_copies[q] = send(pbuf.at[q, other], d2d2.at[q], d2d2_sem, (q,), partner)
+
+    sgn = 1 - 2 * core
+
+    def at(k):
+        return lax.rem(chip + sgn * k + chips, chips)
+
+    names = ("far", "relay", "relay_back", "next", "back", "two", "two_back")
+    slot = {name: i for i, name in enumerate(names)}
+    rs2_copies, ag2_copies, fw2_copies = {}, {}, {}
+
+    def rs_send(q, name, z, k):
+        rs2_copies[q, name] = send(sbuf.at[q, z], rs2.at[q, slot[name]], rs2_sem, (q, slot[name]), at(k) * 2 + core)
+
+    def rs_first(q):
+        d2d2_copies[q].wait_recv()
+        for z in range(chips):
+            sbuf[q, z] = pbuf[q, core, z] + d2d2[q, z]
+        rs_send(q, "far", at(4), 2)
+        rs_send(q, "relay", at(3), 1)
+        rs_send(q, "relay_back", at(-3), -1)
+
+    def rs_direct(q):
+        rs_send(q, "next", at(1), 1)
+        rs_send(q, "back", at(-1), -1)
+
+    def rs_second(q):
+        rs2_copies[q, "relay_back"].wait_recv()
+        sbuf[q, at(-2)] = sbuf[q, at(-2)] + rs2[q, slot["relay_back"]]
+        rs_send(q, "two_back", at(-2), -2)
+        rs2_copies[q, "relay"].wait_recv()
+        rs2_copies[q, "far"].wait_recv()
+        sbuf[q, at(2)] = sbuf[q, at(2)] + rs2[q, slot["relay"]] + rs2[q, slot["far"]]
+        rs_send(q, "two", at(2), 2)
+
+    def ag_send(q, name, z, k):
+        ref = ybuf.at[q, core, z]
+        ag2_copies[q, name] = send(ref, ref, ag2_sem, (q, slot[name]), at(k) * 2 + core)
+
+    def ag_first(q):
+        h, r = q // 2, q % 2
+        total = sbuf[q, chip]
+        for name in ("next", "back", "two_back", "two"):
+            rs2_copies[q, name].wait_recv()
+            total = total + rs2[q, slot[name]]
+        x = xmid[pl.ds(r * rhalf, rhalf), pl.ds(pl.multiple_of(h * hw + me * block, block), block)]
+        ybuf[q, core, chip] = (x + total).astype(BF16).astype(F32)
+        ag_send(q, "two", chip, 2)
+        ag_send(q, "two_back", chip, -2)
+        ag_send(q, "next", chip, 1)
+        ag_send(q, "back", chip, -1)
+        forward2(q, 0, chip)
+
+    def forward2(q, i, z):
+        ref = ybuf.at[q, core, z]
+        fw2_copies[q, i] = send(ref, ref, fw2_sem, (q, i), partner)
+
+    def ag_second(q):
+        ag2_copies[q, "two"].wait_recv()
+        ag_send(q, "far", at(-2), 2)
+        ag_send(q, "relay", at(-2), 1)
+        ag2_copies[q, "two_back"].wait_recv()
+        ag_send(q, "relay_back", at(2), -1)
+        forward2(q, 1, at(-2))
+        forward2(q, 2, at(2))
+        ag2_copies[q, "next"].wait_recv()
+        forward2(q, 3, at(-1))
+        ag2_copies[q, "back"].wait_recv()
+        forward2(q, 4, at(1))
+
+    def ag_third(q):
+        ag2_copies[q, "relay"].wait_recv()
+        forward2(q, 5, at(-3))
+        ag2_copies[q, "relay_back"].wait_recv()
+        forward2(q, 6, at(3))
+        ag2_copies[q, "far"].wait_recv()
+        forward2(q, 7, at(4))
 
     for g in range(GROUPS):
-        for copy in kv_copies[g]:
-            copy.wait()
-
-        @pl.loop(0, nb // 4)
-        def _(i):
-            for j in range(4):
-                attend(g * nb + i * 4 + j)
+        with scope("attend"):
+            for copy in kv_copies[g]:
+                copy.wait()
+
+            @pl.loop(0, nb // 4)
+            def _(i):
+                for j in range(4):
+                    attend(g * nb + i * 4 + j)
 
         if g == 0:
-            pl.semaphore_wait(barrier, chips)
+            with scope("barrier"):
+                pl.semaphore_wait(barrier, chips)
         start_d2d1(g)
         if g > 0:
-            start_rs1(g - 1)
-    start_rs1(GROUPS - 1)
+            with scope("start_rs1"):
+                start_rs1(g - 1)
+    with scope("start_rs1"):
+        start_rs1(GROUPS - 1)
     for g in range(GROUPS):
-        start_ag1(g)
-    wo_copy.wait()
-    for copy in moe_copies:
-        copy.wait()
+        with scope("start_ag1"):
+            start_ag1(g)
+    with scope("weights_wait"):
+        wo_copy.wait()
+        for copy in moe_copies:
+            copy.wait()
     for g in range(GROUPS):
-        forward1(g)
-        finish1(g)
-        project(g)
-        expert_parts(g)
-        start_rs2(g)
-    for g in range(GROUPS):
-        start_ag2(g)
-    for g in range(GROUPS):
-        forward2(g)
-    for g in range(GROUPS):
-        for d in range(chips):
-            fw2_copies[g, d].wait_recv()
-    for z in range(chips):
-        for c in range(2):
-            cols = pl.ds((z * 2 + c) * block, block)
+        with scope("forward1"):
+            forward1(g)
+    with scope("wait_fw1"):
+        for g in range(GROUPS):
+            for d in range(chips):
+                fw1_copies[g, d].wait_recv()
+    with scope("project"):
+        project()
+    with scope("experts"):
+        expert_parts()
+    for stage in (rs_first, rs_direct, rs_second, ag_first, ag_second, ag_third):
+        for q in range(CHUNKS):
+            with scope(stage.__name__):
+                stage(q)
+    with scope("wait_fw2"):
+        for q in range(CHUNKS):
+            for i in range(chips):
+                fw2_copies[q, i].wait_recv()
+    with scope("output"):
+        for h in range(2):
+            for j in range(group):
+                cols = pl.ds(h * hw + j * block, block)
+                y = jnp.concatenate([ybuf[2 * h + r, j % 2, j // 2] for r in range(2)], axis=0).astype(BF16)
+                for s in range(steps):
+                    hidden[s, :, cols] = y[s * batch:(s + 1) * batch]
+    with scope("wait_sends"):
+        for copy in sends:
+            copy.wait_send()
+
+
+def finish_kernel(y, k, v, hidden, tail_k, tail_v):
+    batch, steps, kv_heads, _ = tail_k.shape
+    rows = batch * steps
+    hidden[...] = y[...]
+    for src, dst in ((k, tail_k), (v, tail_v)):
+        for b in range(batch):
             for s in range(steps):
-                parts = [ybuf[g, c, z, pl.ds(s * nb, nb)] for g in range(GROUPS)]
-                hidden[s, :, cols] = jnp.concatenate(parts, axis=0).astype(BF16)
-    for copy in sends:
-        copy.wait_send()
+                dst[b, s] = src[pl.ds(s * batch + b, kv_heads, stride=rows)].astype(BF16)
 
 
 def solution(mesh):
@@ -467,8 +516,8 @@
         keys = shard_len * kv_heads
         nb = batch // GROUPS
         spc = nb // chips
-        rg = steps * nb
-        block = width // group
+        rhalf = rows // 2
+        block = width // group // 2
         kstep = width // K_CHUNKS
         exponent = np.arange(head_dim // 2, dtype=np.float64) * 2.0 / head_dim
         powers = np.tile((ROPE_BASE ** exponent).astype(np.float32), 2)[None]
@@ -502,16 +551,15 @@
             V((2 * half, keys), jnp.int32),
             V((2, batch, half + 8, head_dim), F32), V((batch, half + 8, head_dim), F32), V((batch, half + 8, head_dim), F32),
             V((GROUPS, chips, spc, half + 8, head_dim), F32), V((GROUPS, 2, chips, spc, half, head_dim), F32),
-            V((rg, q_heads * head_dim), F32), V((GROUPS, rg, width), F32), V((rg, width), BF16),
-            V((rg, ff), F32), V((rg, ff), F32),
-            V((GROUPS, 2, chips, rg, block), F32), V((GROUPS, chips, rg, block), F32), V((GROUPS, chips, rg, block), F32),
-            V((GROUPS, chips, rg, block), F32), V((GROUPS, 2, chips, rg, block), F32),
+            V((rows, q_heads * head_dim), F32), V((rows, width), F32), V((rows, width), BF16),
+            V((CHUNKS, 2, chips, rhalf, block), F32), V((CHUNKS, chips, rhalf, block), F32),
+            V((CHUNKS, chips, rhalf, block), F32), V((CHUNKS, 7, rhalf, block), F32), V((CHUNKS, 2, chips, rhalf, block), F32),
             dma((15,)), dma((3, K_CHUNKS)), dma((2, GROUPS)), dma((1,)), dma((3, 2)),
             dma((2, GROUPS)), dma((2, GROUPS, chips)), dma((2, GROUPS, chips)), dma((2, GROUPS, chips)),
-            dma((2, GROUPS)), dma((2, GROUPS, chips)), dma((2, GROUPS, chips)), dma((2, GROUPS, chips)),
+            dma((2, CHUNKS)), dma((2, CHUNKS, 7)), dma((2, CHUNKS, 7)), dma((2, CHUNKS, chips)),
         ]
-        tail_shape = jax.ShapeDtypeStruct((kv_heads, steps, batch, head_dim), BF16)
-        hidden, tail_k, tail_v = pl.pallas_call(
+        tail_shape = jax.ShapeDtypeStruct((kv_heads, rows, head_dim), F32)
+        out = pl.pallas_call(
             functools.partial(kernel, group),
             out_shape=(jax.ShapeDtypeStruct((steps, batch, width), BF16), tail_shape, tail_shape),
             in_specs=in_specs,
@@ -521,8 +569,14 @@
             compiler_params=pltpu.CompilerParams(
                 collective_id=0, has_side_effects=True, vmem_limit_bytes=66_000_000),
         )(*operands)
-        order = (2, 1, 0, 3)
-        return hidden, tail_k.transpose(order), tail_v.transpose(order)
+        final_tail = jax.ShapeDtypeStruct((batch, steps, kv_heads, head_dim), BF16)
+        return pl.pallas_call(
+            finish_kernel,
+            out_shape=(jax.ShapeDtypeStruct((steps, batch, width), BF16), final_tail, final_tail),
+            in_specs=[vmem] * 3,
+            out_specs=(vmem,) * 3,
+            name="finish",
+        )(out[0], out[1].reshape(kv_heads * rows, head_dim), out[2].reshape(kv_heads * rows, head_dim))
 
     replicated = P()
     in_specs = (P('dp'), P(None, 'dp'), P('dp', 'kv'), P('dp', 'kv'), P('dp')) + (replicated,) * 13 + (P(None, None, 'kv'), P(None, None, 'kv'), P(None, 'kv'), replicated, P(None, 'dp'), P(None, 'dp'))

time: 83.1 us -> 71.2 us (0.86)
  Pallas kernels: 77.6 us -> 70.5 us
  local copies, waits for them, and re-layouts: 4.64 us -> 0 us
    pallas_call x1, Pallas kernels: 77.6 us -> 68.6 us  [layer_steps(): pl.pallas_call(functools.partial(kernel, group), out_shape=(jax.ShapeDtyp...]
    unnamed x3 -> x0, local copies, waits for them, and re-layouts: 4.64 us -> none
    pallas_call x0 -> x1, Pallas kernels: none -> 1.91 us  [layer_steps(): pl.pallas_call(finish_kernel, out_shape=(jax.ShapeDtypeStruct((steps, bat...]
where the time goes in v1:
time: 71.2 us; the launch traced here: 71.1 us
  Pallas kernels  70.5 us (99%)
    pallas_call x1, Pallas kernels, layer_steps(): pl.pallas_call(functools.partial(kernel, group), out_shape=(jax.ShapeDtyp...  68.6 us
    pallas_call x1, Pallas kernels, layer_steps(): pl.pallas_call(finish_kernel, out_shape=(jax.ShapeDtypeStruct((steps, bat...  1.91 us

profile of v1, /device:TPU:21, one launch (start us, length us, event | category | flops | bytes accessed | tf_op | source)
XLA Modules:
  0.0 71.1 jit_solution(5461657063297478768)
XLA Ops:
  0.6 68.6 %decode_layer.1 = (bf16[3,16,4096]{2,1,0:T(8,128)(2,1)}, f32[4,48,128]{2,1,0:T(8,128)}, f32[4,48,128]{2,1,0:T(8,128)}) custom-call(bf16[16,4096]{1,0:T(8,128)(2,1)} %x_first.1, bf16[2,16,4096]{2,1,0:T(8,128)(2,1)} %next_emb.1, bf16[16,1024,128]{2,1,0:T(8,128)(2,1)} %bitcast.24, bf16[16,1024,128]{2,1,0:T(8,128)(2,1)} %bitcast.25, s32[16]{0:T(128)} %seq_len.1, ...), custom_call_target="tpu_custom_call" | custom-call | tf_op jit(solution)/shard_map/decode_layer/pallas_call | solution.py:562
  69.2 1.9 %finish.1 = (bf16[3,16,4096]{2,1,0:T(8,128)(2,1)}, bf16[16,3,4,128]{3,2,1,0:T(4,128)(2,1)}, bf16[16,3,4,128]{3,2,1,0:T(4,128)(2,1)}) custom-call(bf16[3,16,4096]{2,1,0:T(8,128)(2,1)} %get-tuple-element.6.y, f32[192,128]{1,0:T(8,128)} %bitcast.30, f32[192,128]{1,0:T(8,128)} %bitcast.31), custom_call_target="tpu_custom_call" | custom-call | tf_op jit(solution)/shard_map/finish/pallas_call | solution.py:573

commit v2 on v1

--- a/solution.py
+++ b/solution.py
@@ -21,6 +21,7 @@
 CHUNKS = 4
 scope = contextlib.nullcontext
 K_CHUNKS = 8
+DEPTH = 5
 TILE = 128
 
 
@@ -50,9 +51,9 @@
     wg, wu, wd, long_factor, powers, idx, mask,
     hidden, tail_k, tail_v,
     xbuf, hbuf, ln1g_v, ln1b_v, ln2g_v, ln2b_v, bo_v, bq_v, bk_v, bv_v, lf_v, pw_v, wr_v, idx_v, mask_v,
-    wq_v, wk_v, wv_v, kc_v, vc_v, wo_v, acc_q, acc_k, acc_v, q2, k2, v2, tcol,
+    wq_v, wk_v, wv_v, kc_v, vc_v, wo_v, wg_v, wu_v, wd_v, acc_q, acc_k, acc_v, q2, k2, v2, tcol, cos_v, sin_v,
     stat, d2d1, rs1_send, rs1, obuf, osum, xmid, h2, pbuf, d2d2, sbuf, rs2, ybuf,
-    small_sem, qkv_sem, kv_sem, wo_sem, moe_sem,
+    small_sem, qkv_sem, kv_sem, wo_sem, moe_sem, ex_sem,
     d2d1_sem, rs1_sem, ag1_sem, fw1_sem, d2d2_sem, rs2_sem, ag2_sem, fw2_sem,
 ):
     batch, width = x_first.shape
@@ -89,10 +90,6 @@
     arrive = sorted(range(1, chips), key=lambda d: min(d, chips - d))
 
     barrier = pltpu.get_barrier_semaphore()
-    pl.semaphore_signal(barrier, inc=1, device_id={"kv": partner}, device_id_type=MESH)
-    for d in order:
-        pl.semaphore_signal(barrier, inc=1, device_id={"kv": peer(d)}, device_id_type=MESH)
-
     smalls = [
         (x_first, xbuf.at[0]), (next_emb, xbuf.at[pl.ds(1, steps - 1)]), (ln1_g, ln1g_v), (ln1_b, ln1b_v),
         (long_factor, lf_v), (powers, pw_v), (bq, bq_v), (bk, bk_v), (bv, bv_v), (bo, bo_v),
@@ -102,19 +99,23 @@
     for copy in small_copies[:6]:
         copy.start()
 
+    q_cols, k_cols = wq_v.shape[2], wk_v.shape[2]
+    q_own = pl.ds(pl.multiple_of(core * q_cols, q_cols), q_cols)
+    k_own = pl.ds(pl.multiple_of(core * k_cols, k_cols), k_cols)
+
     def qkv_copies(k):
-        span = pl.ds(k * kstep, kstep)
+        span = pl.ds(pl.multiple_of(k * kstep, kstep), kstep)
         return [
-            pltpu.make_async_copy(wq.at[span], wq_v.at[k], qkv_sem.at[0, k]),
-            pltpu.make_async_copy(wk.at[span], wk_v.at[k], qkv_sem.at[1, k]),
-            pltpu.make_async_copy(wv.at[span], wv_v.at[k], qkv_sem.at[2, k]),
+            pltpu.make_async_copy(wq.at[span, q_own], wq_v.at[k], qkv_sem.at[0, k]),
+            pltpu.make_async_copy(wk.at[span, k_own], wk_v.at[k], qkv_sem.at[1, k]),
+            pltpu.make_async_copy(wv.at[span, k_own], wv_v.at[k], qkv_sem.at[2, k]),
         ]
 
+    for k in range(DEPTH):
+        for copy in qkv_copies(k):
+            copy.start(priority=1)
     for copy in small_copies[6:]:
         copy.start()
-    for k in range(K_CHUNKS):
-        for copy in qkv_copies(k):
-            copy.start(priority=1)
     kv_copies = []
     for g in range(GROUPS):
         span = pl.ds(g * nb, nb)
@@ -122,19 +123,28 @@
             pltpu.make_async_copy(kc.at[span], kc_v.at[span], kv_sem.at[0, g]),
             pltpu.make_async_copy(vc.at[span], vc_v.at[span], kv_sem.at[1, g]),
         ])
-        for copy in kv_copies[-1]:
-            copy.start(priority=1)
     wo_copy = pltpu.make_async_copy(wo, wo_v, wo_sem.at[0])
-    wo_copy.start(priority=1)
+    moe_copies = [pltpu.make_async_copy(src, dst, moe_sem.at[i]) for i, (src, dst) in enumerate(((wg, wg_v), (wu, wu_v), (wd, wd_v)))]
+    hw = width // 2
+
+    pl.semaphore_signal(barrier, inc=1, device_id={"kv": partner}, device_id_type=MESH)
+    for d in order:
+        pl.semaphore_signal(barrier, inc=1, device_id={"kv": peer(d)}, device_id_type=MESH)
+
+    for copy in small_copies[:6]:
+        copy.wait()
+    for s in range(steps):
+        hbuf[s] = layer_norm_rows(xbuf[s].astype(F32), ln1g_v[...], ln1b_v[...])
+
+    acc_q[...] = jnp.zeros_like(acc_q)
+    acc_k[...] = jnp.zeros_like(acc_k)
+    acc_v[...] = jnp.zeros_like(acc_v)
 
     row_k = iota((qrows, keys), 0)
     col_k = iota((qrows, keys), 1)
     head_of_row = (row_k * 43) >> 9
     pos = me * shard_len + (col_k >> 2)
     tcol[...] = jnp.where(head_of_row == (col_k & 3), pos, jnp.int32(1 << 30))
-
-    for copy in small_copies[:6]:
-        copy.wait()
     lane = iota((batch, TILE), 1)
     sub = iota((batch, TILE), 0)
     lens = jnp.zeros((batch, TILE), jnp.int32)
@@ -143,57 +153,74 @@
     lf = jnp.concatenate([lf_v[...], lf_v[...]], axis=1)
     inv_freq = 1.0 / (lf * pw_v[...])
     sign = jnp.where(lane < TILE // 2, -1.0, 1.0)
-    cos_parts, sin_parts = [], []
     for s in range(steps):
         angles = (lens + s).astype(F32) * inv_freq
-        cos_parts.append(jnp.cos(angles) * ROPE_MSCALE)
-        sin_parts.append(jnp.sin(angles) * ROPE_MSCALE * sign)
-    cos_full = jnp.concatenate(cos_parts, axis=0)
-    sin_full = jnp.concatenate(sin_parts, axis=0)
-
-    for s in range(steps):
-        hbuf[s] = layer_norm_rows(xbuf[s].astype(F32), ln1g_v[...], ln1b_v[...])
-
-    acc_q[...] = jnp.zeros_like(acc_q)
-    acc_k[...] = jnp.zeros_like(acc_k)
-    acc_v[...] = jnp.zeros_like(acc_v)
+        cos_v[pl.ds(s * batch, batch)] = jnp.cos(angles) * ROPE_MSCALE
+        sin_v[pl.ds(s * batch, batch)] = jnp.sin(angles) * ROPE_MSCALE * sign
 
     @pl.loop(0, K_CHUNKS)
     def _(k):
         for copy in qkv_copies(k):
             copy.wait()
+
+        @pl.when(k + DEPTH < K_CHUNKS)
+        def _():
+            for copy in qkv_copies(k + DEPTH):
+                copy.start(priority=1)
+
+        for g in range(GROUPS):
+            @pl.when(k == K_CHUNKS - DEPTH + 2 * g)
+            def _():
+                for copy in kv_copies[g]:
+                    copy.start(priority=1)
+
         h = hbuf[:, :, pl.ds(pl.multiple_of(k * kstep, kstep), kstep)].reshape(rows, kstep)
         acc_q[...] += dot_nn(h, wq_v[k])
         acc_k[...] += dot_nn(h, wk_v[k])
         acc_v[...] += dot_nn(h, wv_v[k])
 
-    moe_copies = []
-    hw = width // 2
-    for i, src in enumerate((wg, wu, wd)):
-        for j in range(2):
-            copy = pltpu.make_async_copy(src.at[:, pl.ds(j * hw, hw)], wq_v.at[2 * i + j, pl.ds(0, ff)], moe_sem.at[i, j])
-            copy.start(priority=1)
-            moe_copies.append(copy)
+    wo_copy.start(priority=1)
     for copy in small_copies[6:]:
         copy.wait()
 
+    sends = []
+
+    def send(src, dst, sems, slot, device):
+        copy = pltpu.make_async_remote_copy(
+            src_ref=src, dst_ref=dst, send_sem=sems.at[(0,) + slot], recv_sem=sems.at[(1,) + slot],
+            device_id={"kv": device}, device_id_type=MESH)
+        copy.start()
+        sends.append(copy)
+        return copy
+
     def rotate(x):
         x = x.astype(BF16).astype(F32)
-        return (x * cos_full + pltpu.roll(x, TILE // 2, 1) * sin_full).astype(BF16).astype(F32)
-
-    for i in range(q_heads):
+        return (x * cos_v[...] + pltpu.roll(x, TILE // 2, 1) * sin_v[...]).astype(BF16).astype(F32)
+
+    q_span = pl.ds(pl.multiple_of(core * (q_heads // 2 * rows), rows), q_heads // 2 * rows)
+    k_span = pl.ds(pl.multiple_of(core * (kv_heads // 2 * rows), rows), kv_heads // 2 * rows)
+
+    def head_rows(i, per):
+        return pl.ds(pl.multiple_of((core * per + i) * rows, rows), rows)
+
+    def head_cols(i, per):
+        return pl.ds(pl.multiple_of((core * per + i) * TILE, TILE), TILE)
+
+    half_q, half_kv = q_heads // 2, kv_heads // 2
+    for i in range(half_q):
+        q2[head_rows(i, half_q)] = rotate(acc_q[:, pl.ds(i * TILE, TILE)] + bq_v[:, head_cols(i, half_q)])
+    with scope("barrier"):
+        pl.semaphore_wait(barrier, chips)
+    exchanges = [send(q2.at[q_span], q2.at[q_span], ex_sem, (0,), partner)]
+    for i in range(half_kv):
         cols = pl.ds(i * TILE, TILE)
-        q2[pl.ds(i * rows, rows)] = rotate(acc_q[:, cols] + bq_v[:, cols])
-    for i in range(kv_heads):
-        cols = pl.ds(i * TILE, TILE)
-        k_rot = rotate(acc_k[:, cols] + bk_v[:, cols])
-        v_new = (acc_v[:, cols] + bv_v[:, cols]).astype(BF16)
-        k2[pl.ds(i * rows, rows)] = k_rot
-        v2[pl.ds(i * rows, rows)] = v_new.astype(F32)
-        tail_k[i] = k_rot
-        tail_v[i] = v_new.astype(F32)
-    k2[pl.ds(kv_heads * rows, k2.shape[0] - kv_heads * rows)] = jnp.zeros((k2.shape[0] - kv_heads * rows, TILE), F32)
-    v2[pl.ds(kv_heads * rows, v2.shape[0] - kv_heads * rows)] = jnp.zeros((v2.shape[0] - kv_heads * rows, TILE), F32)
+        k2[head_rows(i, half_kv)] = rotate(acc_k[:, cols] + bk_v[:, head_cols(i, half_kv)])
+        v2[head_rows(i, half_kv)] = (acc_v[:, cols] + bv_v[:, head_cols(i, half_kv)]).astype(BF16).astype(F32)
+    exchanges.append(send(k2.at[k_span], k2.at[k_span], ex_sem, (1,), partner))
+    exchanges.append(send(v2.at[k_span], v2.at[k_span], ex_sem, (2,), partner))
+    pad = pl.ds(kv_heads * rows, k2.shape[0] - kv_heads * rows)
+    k2[pad] = jnp.zeros((k2.shape[0] - kv_heads * rows, TILE), F32)
+    v2[pad] = jnp.zeros((v2.shape[0] - kv_heads * rows, TILE), F32)
 
     eye = iota((half, TILE), 0) == iota((half, TILE), 1)
     sub8 = iota((8, TILE), 0)
@@ -220,16 +247,6 @@
             part = slice(hf * half, (hf + 1) * half)
             stat[hf, b, pl.ds(0, half)] = out[part]
             stat[hf, b, pl.ds(half, 8)] = pair_tile(to_row(top[part]), to_row(total[part]))
-
-    sends = []
-
-    def send(src, dst, sems, slot, device):
-        copy = pltpu.make_async_remote_copy(
-            src_ref=src, dst_ref=dst, send_sem=sems.at[(0,) + slot], recv_sem=sems.at[(1,) + slot],
-            device_id={"kv": device}, device_id_type=MESH)
-        copy.start()
-        sends.append(copy)
-        return copy
 
     d2d1_copies, rs1_copies, ag1_copies, fw1_copies = {}, {}, {}, {}
     d2d2_copies = {}
@@ -344,12 +361,11 @@
 
     def expert_parts():
         gate = gates()
-        span = pl.ds(0, ff)
-        ag = dot_nt(h2[:, :hw], wq_v[0, span]) + dot_nt(h2[:, hw:], wq_v[1, span])
-        au = dot_nt(h2[:, :hw], wq_v[2, span]) + dot_nt(h2[:, hw:], wq_v[3, span])
+        ag = dot_nt(h2[...], wg_v[...])
+        au = dot_nt(h2[...], wu_v[...])
         u = (gate * (ag * (1.0 / (1.0 + jnp.exp(-ag)))) * au).astype(BF16)
         for h in range(2):
-            part = dot_nn(u, wq_v[4 + h, span]).astype(BF16).astype(F32)
+            part = dot_nn(u, wd_v[:, pl.ds(h * hw, hw)]).astype(BF16).astype(F32)
             for j in range(group):
                 for r in range(2):
                     pbuf[2 * h + r, j % 2, j // 2] = part[r * rhalf:(r + 1) * rhalf, j * block:(j + 1) * block]
@@ -433,23 +449,33 @@
         ag2_copies[q, "far"].wait_recv()
         forward2(q, 7, at(4))
 
+    def attend_span(first, count):
+        @pl.loop(0, count // 4)
+        def _(i):
+            for j in range(4):
+                attend(first + i * 4 + j)
+
+    with scope("wait_exchange"):
+        for copy in exchanges:
+            copy.wait_recv()
     for g in range(GROUPS):
-        with scope("attend"):
-            for copy in kv_copies[g]:
-                copy.wait()
-
-            @pl.loop(0, nb // 4)
-            def _(i):
-                for j in range(4):
-                    attend(g * nb + i * 4 + j)
-
+        for copy in kv_copies[g]:
+            copy.wait()
         if g == 0:
-            with scope("barrier"):
-                pl.semaphore_wait(barrier, chips)
-        start_d2d1(g)
-        if g > 0:
+            with scope("attend"):
+                attend_span(0, nb)
+            for copy in moe_copies:
+                copy.start(priority=1)
+        else:
+            with scope("attend"):
+                attend_span(g * nb, nb // 2)
             with scope("start_rs1"):
                 start_rs1(g - 1)
+            with scope("attend"):
+                attend_span(g * nb + nb // 2, nb // 2)
+        start_d2d1(g)
+    tail_k[...] = k2[pl.ds(0, kv_heads * rows)]
+    tail_v[...] = v2[pl.ds(0, kv_heads * rows)]
     with scope("start_rs1"):
         start_rs1(GROUPS - 1)
     for g in range(GROUPS):
@@ -543,22 +569,23 @@
             V((1, q_heads * head_dim), F32), V((1, kv_heads * head_dim), F32), V((1, kv_heads * head_dim), F32),
             V((1, head_dim // 2), F32), V((1, head_dim), F32), V((experts, width), BF16),
             V((steps, expert_idx.shape[2], batch), jnp.int32), V(route_mask.shape, jnp.int32),
-            V((K_CHUNKS, kstep, q_heads * head_dim), BF16),
-            V((K_CHUNKS, kstep, kv_heads * head_dim), BF16), V((K_CHUNKS, kstep, kv_heads * head_dim), BF16),
+            V((K_CHUNKS, kstep, q_heads * head_dim // 2), BF16),
+            V((K_CHUNKS, kstep, kv_heads * head_dim // 2), BF16), V((K_CHUNKS, kstep, kv_heads * head_dim // 2), BF16),
             V((batch, keys, head_dim), BF16), V((batch, keys, head_dim), BF16), V(w_o.shape, BF16),
-            V((rows, q_heads * head_dim), F32), V((rows, kv_heads * head_dim), F32), V((rows, kv_heads * head_dim), F32),
+            V((ff, width), BF16), V((ff, width), BF16), V((ff, width), BF16),
+            V((rows, q_heads * head_dim // 2), F32), V((rows, kv_heads * head_dim // 2), F32), V((rows, kv_heads * head_dim // 2), F32),
             V((q_heads * rows, head_dim), F32), V((16 * batch, head_dim), F32), V((16 * batch, head_dim), F32),
-            V((2 * half, keys), jnp.int32),
+            V((2 * half, keys), jnp.int32), V((rows, head_dim), F32), V((rows, head_dim), F32),
             V((2, batch, half + 8, head_dim), F32), V((batch, half + 8, head_dim), F32), V((batch, half + 8, head_dim), F32),
             V((GROUPS, chips, spc, half + 8, head_dim), F32), V((GROUPS, 2, chips, spc, half, head_dim), F32),
             V((rows, q_heads * head_dim), F32), V((rows, width), F32), V((rows, width), BF16),
             V((CHUNKS, 2, chips, rhalf, block), F32), V((CHUNKS, chips, rhalf, block), F32),
             V((CHUNKS, chips, rhalf, block), F32), V((CHUNKS, 7, rhalf, block), F32), V((CHUNKS, 2, chips, rhalf, block), F32),
-            dma((15,)), dma((3, K_CHUNKS)), dma((2, GROUPS)), dma((1,)), dma((3, 2)),
+            dma((15,)), dma((3, K_CHUNKS)), dma((2, GROUPS)), dma((1,)), dma((3,)), dma((2, 3)),
             dma((2, GROUPS)), dma((2, GROUPS, chips)), dma((2, GROUPS, chips)), dma((2, GROUPS, chips)),
             dma((2, CHUNKS)), dma((2, CHUNKS, 7)), dma((2, CHUNKS, 7)), dma((2, CHUNKS, chips)),
         ]
-        tail_shape = jax.ShapeDtypeStruct((kv_heads, rows, head_dim), F32)
+        tail_shape = jax.ShapeDtypeStruct((kv_heads * rows, head_dim), F32)
         out = pl.pallas_call(
             functools.partial(kernel, group),
             out_shape=(jax.ShapeDtypeStruct((steps, batch, width), BF16), tail_shape, tail_shape),
@@ -576,7 +603,7 @@
             in_specs=[vmem] * 3,
             out_specs=(vmem,) * 3,
             name="finish",
-        )(out[0], out[1].reshape(kv_heads * rows, head_dim), out[2].reshape(kv_heads * rows, head_dim))
+        )(*out)
 
     replicated = P()
     in_specs = (P('dp'), P(None, 'dp'), P('dp', 'kv'), P('dp', 'kv'), P('dp')) + (replicated,) * 13 + (P(None, None, 'kv'), P(None, None, 'kv'), P(None, 'kv'), replicated, P(None, 'dp'), P(None, 'dp'))

time: 71.2 us -> 65.2 us (0.916)
  Pallas kernels: 70.5 us -> 64.5 us
    pallas_call x1, Pallas kernels: 68.6 us -> 62.5 us  [layer_steps(): pl.pallas_call(functools.partial(kernel, group), out_shape=(jax.ShapeDtyp...]
where the time goes in v2:
time: 65.2 us; the launch traced here: 65.1 us
  Pallas kernels  64.5 us (99%)
    pallas_call x1, Pallas kernels, layer_steps(): pl.pallas_call(functools.partial(kernel, group), out_shape=(jax.ShapeDtyp...  62.5 us
    pallas_call x1, Pallas kernels, layer_steps(): pl.pallas_call(finish_kernel, out_shape=(jax.ShapeDtypeStruct((steps, bat...  1.91 us

profile of v2, /device:TPU:21, one launch (start us, length us, event | category | flops | bytes accessed | tf_op | source)
XLA Modules:
  0.0 65.1 jit_solution(1428528723467044685)
XLA Ops:
  0.6 62.5 %decode_layer.1 = (bf16[3,16,4096]{2,1,0:T(8,128)(2,1)}, f32[192,128]{1,0:T(8,128)}, f32[192,128]{1,0:T(8,128)}) custom-call(bf16[16,4096]{1,0:T(8,128)(2,1)} %x_first.1, bf16[2,16,4096]{2,1,0:T(8,128)(2,1)} %next_emb.1, bf16[16,1024,128]{2,1,0:T(8,128)(2,1)} %bitcast.22, bf16[16,1024,128]{2,1,0:T(8,128)(2,1)} %bitcast.23, s32[16]{0:T(128)} %seq_len.1, ...), custom_call_target="tpu_custom_call" | custom-call | tf_op jit(solution)/shard_map/decode_layer/pallas_call | solution.py:589
  63.2 1.9 %finish.1 = (bf16[3,16,4096]{2,1,0:T(8,128)(2,1)}, bf16[16,3,4,128]{3,2,1,0:T(4,128)(2,1)}, bf16[16,3,4,128]{3,2,1,0:T(4,128)(2,1)}) custom-call(bf16[3,16,4096]{2,1,0:T(8,128)(2,1)} %get-tuple-element.6.y, f32[192,128]{1,0:T(8,128)} %get-tuple-element.7.k, f32[192,128]{1,0:T(8,128)} %get-tuple-element.8.v), custom_call_target="tpu_custom_call" | custom-call | tf_op jit(solution)/shard_map/finish/pallas_call | solution.py:600
